TPU v7x, 32 devices: a whole 2x2x4 slice. The times are simulated.
32 devices in a mesh: rows: 4 (over y, core), cols: 8 (over z, x).
Axes of the slice: x: 2, y: 2, z: 4, core: 2. Of those that a mesh axis runs over, the one named last changes fastest.
Arguments:
- single: bfloat16 [512, 1024], P('rows'), may hold values from -6 to 6
- pair: bfloat16 [512, 512, 128], P('rows', 'cols'), may hold values from -6 to 6
- residue_mask: int32 [512], replicated, may hold values from 0 to 1, as said below
- w_bias: bfloat16 [128, 32], replicated, may hold values from -40 to 40
- w_project: bfloat16 [4, 1024, 1024], P(None, None, 'cols'), may hold values from -0.1875 to 0.1875
- w_out: bfloat16 [1024, 1024], replicated, may hold values from -0.1875 to 0.1875
- w_factors: bfloat16 [1024, 128], replicated, may hold values from -0.1875 to 0.1875
- w_pairout: bfloat16 [128, 128], replicated, may hold values from -0.5 to 0.5
- w_up: bfloat16 [128, 512], replicated, may hold values from -0.5 to 0.5
- w_down: bfloat16 [512, 128], replicated, may hold values from -0.25 to 0.25
Outputs:
- single_out: bfloat16 [512, 1024], P('rows')
- pair_out: bfloat16 [512, 512, 128], P('rows', 'cols')
Inputs may be any that keep to these rules, and one draw needn't show every extreme that they name: residue_mask is 1 on a leading run of at least 256 positions and 0 after it.
All inputs are finite; a program needn't handle non-finite values.
Results may differ from a plain program's by a relative error of at most 0.01.
The roundings to bfloat16 on the way count: a program that leaves them out, or rounds other values in their place, can miss the bound.
Values may be sent and summed in bfloat16 or wider, within the bound.
A program may use at most 64 MiB of HBM per device.

v0:
```python
import math

import jax
import jax.numpy as jnp
from jax import lax
from jax.sharding import PartitionSpec as P

epsilon = 1e-05


def from_root(value, axis, root):
    mine = lax.axis_index(axis) == root
    return lax.psum(jnp.where(mine, value, jnp.zeros_like(value)), axis)


def layer_norm(values):
    values = values.astype(jnp.float32)
    centred = values - jnp.mean(values, -1, keepdims=True)
    return centred * lax.rsqrt(jnp.mean(centred * centred, -1, keepdims=True) + epsilon)


def per_device(
    single, pair, residue_mask, w_bias, w_project, w_out, w_factors, w_pairout, w_up, w_down
):
    tile_rows = pair.shape[0]
    tile_cols = pair.shape[1]
    normed_pair = layer_norm(pair).astype(jnp.bfloat16)
    bias_local = jnp.einsum(
        "rcp,ph->hrc", normed_pair, w_bias, preferred_element_type=jnp.float32
    ).astype(jnp.bfloat16)
    normed_single = layer_norm(single).astype(jnp.bfloat16)
    projected = jnp.einsum(
        "rs,fsc->frc", normed_single, w_project, preferred_element_type=jnp.float32
    )
    query_rows = projected[0].astype(jnp.bfloat16)
    key_local = projected[1].astype(jnp.bfloat16)
    value_local = projected[2].astype(jnp.bfloat16)
    gate_values = jax.nn.sigmoid(projected[3])
    first_residue = lax.axis_index("cols") * tile_cols
    owner_row = first_residue // tile_rows
    offset_rows = first_residue - owner_row * tile_rows
    bias_heads = lax.all_to_all(bias_local, "cols", split_axis=0, concat_axis=2, tiled=True)
    key_rows, value_rows = (
        lax.all_gather(key_local, "rows", axis=0, tiled=True),
        lax.all_gather(value_local, "rows", axis=0, tiled=True),
    )
    heads_here = bias_heads.shape[0]
    head_width = query_rows.shape[1] // heads_here
    residues = key_rows.shape[0]
    query_split = query_rows.reshape(tile_rows, heads_here, head_width)
    key_split = key_rows.reshape(residues, heads_here, head_width)
    value_split = value_rows.reshape(residues, heads_here, head_width)
    score_scale = 1.0 / math.sqrt(head_width)
    scores = jnp.einsum(
        "rhd,lhd->hrl", query_split, key_split, preferred_element_type=jnp.float32
    ) * score_scale + bias_heads.astype(jnp.float32)
    key_valid = (residue_mask > 0)[None, None, :]
    scores = jnp.where(key_valid, scores, -jnp.inf)
    weights = jax.nn.softmax(scores, axis=-1).astype(jnp.bfloat16)
    attended = jnp.einsum("hrl,lhd->rhd", weights, value_split, preferred_element_type=jnp.float32)
    attended = attended.reshape(tile_rows, heads_here * head_width)
    mixed = (attended * gate_values).astype(jnp.bfloat16)
    whole_heads = lax.all_gather(mixed, "cols", axis=1, tiled=True)
    head_total = jnp.dot(whole_heads, w_out, preferred_element_type=jnp.float32)
    single_out = (single.astype(jnp.float32) + head_total).astype(jnp.bfloat16)
    normed_out = layer_norm(single_out).astype(jnp.bfloat16)
    factors = jnp.dot(normed_out, w_factors, preferred_element_type=jnp.float32).astype(
        jnp.bfloat16
    )
    factor_width = factors.shape[1] // 2
    left_factor = factors[:, :factor_width]
    right_local = factors[:, factor_width:]
    right_piece = lax.dynamic_slice_in_dim(right_local, offset_rows, tile_cols, 0)
    right_cols = from_root(right_piece, "rows", owner_row)
    block_rows = math.gcd(tile_rows, max(1, 4096 // tile_cols))
    count_blocks = tile_rows // block_rows

    def update_block(operands):
        pair_block, left_block = operands
        left_wide = left_block.astype(jnp.float32)[:, None, :]
        right_wide = right_cols.astype(jnp.float32)[None, :, :]
        paired = jnp.concatenate([left_wide * right_wide, left_wide - right_wide], -1).astype(
            jnp.bfloat16
        )
        pair_mid = (
            pair_block.astype(jnp.float32)
            + jnp.einsum("rcq,qp->rcp", paired, w_pairout, preferred_element_type=jnp.float32)
        ).astype(jnp.bfloat16)
        normed_mid = layer_norm(pair_mid).astype(jnp.bfloat16)
        hidden = jax.nn.relu(
            jnp.einsum("rcp,pk->rck", normed_mid, w_up, preferred_element_type=jnp.float32)
        ).astype(jnp.bfloat16)
        return (
            pair_mid.astype(jnp.float32)
            + jnp.einsum("rck,kp->rcp", hidden, w_down, preferred_element_type=jnp.float32)
        ).astype(jnp.bfloat16)

    updated = lax.map(
        update_block,
        (
            pair.reshape(count_blocks, block_rows, tile_cols, pair.shape[2]),
            left_factor.reshape(count_blocks, block_rows, factor_width),
        ),
    )
    return (single_out, updated.reshape(pair.shape))


def solution(mesh):
    return jax.shard_map(
        per_device,
        mesh=mesh,
        in_specs=(
            P("rows", None),
            P("rows", "cols", None),
            P(),
            P(),
            P(None, None, "cols"),
            P(),
            P(),
            P(),
            P(),
            P(),
        ),
        out_specs=(P("rows", None), P("rows", "cols", None)),
        check_vma=False,
    )
```

profile of v0, /device:TPU:0, one launch (start us, length us, event | category | flops | bytes accessed | tf_op | source)
XLA Modules:
  0.0 100.3 jit_solution(4183967973226425376)
XLA Ops:
  0.6 0.0 copy-start
  0.6 0.0 copy-start.1
  0.7 2.9 %convert_reduce_fusion.1 = f32[128,64]{1,0:T(8,128)S(1)} fusion(bf16[128,64,128]{2,1,0:T(8,128)(2,1)} %param.13), kind=kLoop, calls=%fused_computation.33 | loop fusion | flops 2088960 | bytes 2129920 | tf_op jit(solution)/shard_map/reduce_sum | solution.py:18
  3.6 2.7 %fusion.30 = f32[128,64]{1,0:T(8,128)S(1)} fusion(bf16[128,64,128]{2,1,0:T(8,128)(2,1)S(1)} %copy-done.1, f32[128,64]{1,0:T(8,128)S(1)} %broadcast_multiply_fusion.1), kind=kLoop, calls=%fused_computation.36 | loop fusion | flops 4186112 | bytes 2162688 | tf_op jit(solution)/shard_map/reduce_sum | solution.py:19
  6.4 0.0 copy-start.7
  6.4 3.4 %fusion.31 = bf16[128,64,128]{2,1,0:T(8,128)(2,1)S(1)} fusion(bf16[128,64,128]{2,1,0:T(8,128)(2,1)S(1)} %copy-done.1, f32[128,64]{1,0:T(8,128)S(1)} %add_rsqrt_fusion.1, f32[128,64]{1,0:T(8,128)S(1)} %broadcast_multiply_fusion.1), kind=kLoop, calls=%fused_computation.37 | loop fusion | flops 4194304 | bytes 4259840 | tf_op jit(solution)/shard_map/convert_element_type | solution.py:27
  9.7 0.0 copy-start.3
  9.8 1.4 %fusion.41 = bf16[32,128,64]{1,0,2:T(8,128)(2,1)S(1)} fusion(bf16[128,64,128]{2,1,0:T(8,128)(2,1)S(1)} %fusion.31, bf16[128,32]{0,1:T(8,128)(2,1)S(1)} %copy-done.7), kind=kOutput, calls=%fused_computation.46 | convolution fusion | flops 67371008 | bytes 2629632 | tf_op jit(solution)/shard_map/rcp,ph->hrc/dot_general | solution.py:28
  11.1 1.0 %copy.31 = bf16[32,128,64]{1,2,0:T(8,128)(2,1)} copy(bf16[32,128,64]{1,0,2:T(8,128)(2,1)S(1)} %fusion.41) | data formatting | bytes 1048576 | tf_op jit(solution)/shard_map/convert_element_type | solution.py:30
  12.2 7.3 %all-to-all-start = ((bf16[32,128,64]{1,2,0:T(8,128)(2,1)}), bf16[32,128,64]{1,2,0:T(8,128)(2,1)}, u32[]{:S(2)}, u32[]{:S(2)}) async-start(bf16[32,128,64]{1,2,0:T(8,128)(2,1)} %copy.31), calls=%async_computation | async-start | bytes 1048576 | tf_op jit(solution)/shard_map/all_to_all | solution.py:42
  19.5 0.1 convert_reduce_fusion.2
  19.6 0.2 fusion.49
  19.9 1.5 %copy.29 = bf16[4,1024,128]{1,2,0:T(8,128)(2,1)S(1)} copy(bf16[4,1024,128]{2,1,0:T(8,128)(2,1)} %param.16) | data formatting | bytes 2097152 | tf_op args[4]
  21.3 0.5 fusion.55
  21.9 0.0 copy-start.4
  21.9 0.7 copy-done.4
  22.6 0.6 fusion.69
  23.2 5.4 %all-gather.1 = bf16[1,512,128]{1,2,0:T(8,128)(2,1)S(1)} all-gather(bf16[1,128,128]{1,2,0:T(8,128)(2,1)S(1)} %get-tuple-element.97), channel_id=3, replica_groups=mesh['rows'=4,'cols'=8] {'rows'}, dimensions={1}, use_global_device_ids=true | all-gather | bytes 163840 | tf_op jit(solution)/shard_map/all_gather | solution.py:44
  28.7 5.9 %all-gather = bf16[1,512,128]{1,2,0:T(8,128)(2,1)} all-gather(bf16[1,128,128]{1,2,0:T(8,128)(2,1)S(1)} %get-tuple-element.99), channel_id=2, replica_groups=mesh['rows'=4,'cols'=8] {'rows'}, dimensions={1}, use_global_device_ids=true | all-gather | bytes 163840 | tf_op jit(solution)/shard_map/all_gather | solution.py:45
  34.5 1.1 %convert_bitcast_fusion = f32[4,128,8,64]{1,3,0,2:T(8,128)S(1)} fusion(bf16[8,4,128,64]{2,3,1,0:T(8,128)(2,1)} %bitcast.28), kind=kLoop, calls=%fused_computation.50 | loop fusion | flops 262144 | bytes 1572864 | tf_op jit(solution)/shard_map/convert_element_type | solution.py:56
  35.7 0.1 copy.32
  35.8 1.3 %copy.33 = f32[4,128,512]{2,1,0:T(8,128)} copy(f32[4,128,512]{1,2,0:T(8,128)S(1)} %bitcast.77) | data formatting | bytes 2097152 | tf_op jit(solution)/shard_map/convert_element_type | solution.py:56
  37.1 1.6 %fusion.37 = f32[4,128,512]{2,1,0:T(8,128)S(1)} fusion(f32[4,128,512]{2,1,0:T(8,128)} %copy.33, bf16[128,4,32]{0,2,1:T(8,128)(2,1)} %bitcast.82, bf16[512,4,32]{0,2,1:T(8,128)(2,1)S(1)} %bitcast.80, pred[512]{0:T(512)(128)(4,1)S(1)} %broadcast_compare_fusion), kind=kOutput, calls=%fused_computation.44 | convolution fusion | flops 17563648 | bytes 2261504 | tf_op jit(solution)/shard_map/rhd,lhd->hrl/dot_general | solution.py:54
  38.7 0.3 fusion.71
  39.0 1.9 %fusion.53 = f32[4,32,128]{2,1,0:T(8,128)S(1)} fusion(bf16[512,4,32]{0,2,1:T(8,128)(2,1)} %bitcast.83, f32[4,128]{1,0:T(4,128)S(1)} %fusion.71, f32[4,128,512]{2,1,0:T(8,128)S(1)} %fusion.37), kind=kOutput, calls=%fused_computation.64 | convolution fusion | flops 17564672 | bytes 1247232 | tf_op jit(solution)/shard_map/hrl,lhd->rhd/dot_general | solution.py:60
  41.0 0.9 fusion.66
  41.9 0.0 copy-start.6
  41.9 0.0 copy-start.10
  41.9 31.5 %all_gather.11 = bf16[128,1024]{0,1:T(8,128)(2,1)S(1)} all-gather(bf16[128,128]{0,1:T(8,128)(2,1)S(1)} %fusion.66), channel_id=1, replica_groups=mesh['rows'=4,'cols'=8] {'cols'}, dimensions={1}, use_global_device_ids=true | all-gather | bytes 294912 | tf_op jit(solution)/shard_map/all_gather | solution.py:63
  73.4 0.5 convert_reduce_fusion.3
  74.0 0.2 fusion.51
  74.2 0.3 convolution_convert_fusion
  74.6 0.1 dynamic-slice_select_fusion
  74.7 10.3 %psum.7 = bf16[64,64]{0,1:T(8,128)(2,1)S(1)} all-reduce(bf16[64,64]{0,1:T(8,128)(2,1)S(1)} %dynamic-slice_select_fusion), channel_id=1, replica_groups=mesh['rows'=4,'cols'=8] {'rows'}, use_global_device_ids=true, to_apply=%region_8.9 | all-reduce | flops 4096 | bytes 16384 | tf_op jit(solution)/shard_map/psum | solution.py:13
  85.0 0.1 copy.35
  85.1 0.1 copy.36
  85.2 15.0 %while.10 = (s32[]{:T(128)}, bf16[2,64,64,128]{3,2,1,0:T(8,128)(2,1)}, bf16[2,64,64,128]{3,2,1,0:T(8,128)(2,1)}, bf16[2,64,64]{2,1,0:T(8,128)(2,1)S(1)}, bf16[64...) while((s32[]{:T(128)}, ...), condition=%wide.region_12.13_spmd, body=%wide.region_9.12_spmd.sunk | while | flops 1223700480 | bytes 17334912 | solution.py:98
  85.2 0.0 copy-start.2
  85.3 0.5 multiply_convert_fusion.2
  85.8 1.0 copy-done.2
  86.8 1.2 %convert_reduce_fusion.5 = (f32[64,64]{1,0:T(8,128)S(1)}, bf16[64,64,128]{2,1,0:T(8,128)(2,1)S(1)}) fusion(bf16[128,128]{1,0:T(8,128)(2,1)S(1)} %get-tuple-element.184, bf16[64,64,64]{2,1,0:T(8,128)(2,1)S(1)} %get-tuple-element.157, bf16[64,64,64]{2,1,0:T(8,128)(2,1)S(1)} %get-tuple-element.158, bf16[2,64,64,128]{3,2,1,0:T(8,128)(2,1)S(1)} %copy-done.2, ...), kind=kOutput, calls=%fused_computation.6.clone.1 | convolution fusion | flops 138932224 | bytes 3194884 | tf_op jit(solution)/shard_map/while/body/eval_jaxpr/rcq,qp->rcp/dot_general | solution.py:87
  88.1 1.3 %fusion.89 = f32[64,64]{1,0:T(8,128)S(1)} fusion(bf16[64,64,128]{2,1,0:T(8,128)(2,1)S(1)} %get-tuple-element.159, f32[64,64]{1,0:T(8,128)S(1)} %broadcast_multiply_fusion.5), kind=kLoop, calls=%fused_computation.9.clone.1 | loop fusion | flops 2093056 | bytes 1081344 | tf_op jit(solution)/shard_map/while/body/eval_jaxpr/reduce_sum | solution.py:19
  89.4 3.4 %fusion.90 = bf16[2,64,64,128]{3,2,1,0:T(8,128)(2,1)} fusion(bf16[2,64,64,128]{3,2,1,0:T(8,128)(2,1)} %get-tuple-element.171, s32[]{:T(128)} %get-tuple-element.170, bf16[64,64,128]{2,1,0:T(8,128)(2,1)S(1)} %get-tuple-element.159, f32[64,64]{1,0:T(8,128)S(1)} %add_rsqrt_fusion.5, f32[64,64]{1,0:T(8,128)S(1)} %broadcast_multiply_fusion.5, ...), kind=kOutput, calls=%fused_computation.17.clone.1 | convolution fusion | flops 1081606144 | bytes 3473920 | tf_op jit(solution)/shard_map/while/body/eval_jaxpr/rck,kp->rcp/dot_general | solution.py:95
  92.8 0.5 multiply_convert_fusion.2
  93.3 1.0 %copy-done.2 = bf16[2,64,64,128]{3,2,1,0:T(8,128)(2,1)S(1)} copy-done((bf16[2,64,64,128]{3,2,1,0:T(8,128)(2,1)S(1)}, bf16[2,64,64,128]{3,2,1,0:T(8,128)(2,1)}, u32[]{:S(2)}) %copy-start.2) | copy-done | bytes 2097176 | tf_op jit(solution)/shard_map/while
  94.4 1.2 %convert_reduce_fusion.5 = (f32[64,64]{1,0:T(8,128)S(1)}, bf16[64,64,128]{2,1,0:T(8,128)(2,1)S(1)}) fusion(bf16[128,128]{1,0:T(8,128)(2,1)S(1)} %get-tuple-element.184, bf16[64,64,64]{2,1,0:T(8,128)(2,1)S(1)} %get-tuple-element.157, bf16[64,64,64]{2,1,0:T(8,128)(2,1)S(1)} %get-tuple-element.158, bf16[2,64,64,128]{3,2,1,0:T(8,128)(2,1)S(1)} %copy-done.2, ...), kind=kOutput, calls=%fused_computation.6.clone.1 | convolution fusion | flops 138932224 | bytes 3194884 | tf_op jit(solution)/shard_map/while/body/eval_jaxpr/rcq,qp->rcp/dot_general | solution.py:87
  95.6 1.3 %fusion.89 = f32[64,64]{1,0:T(8,128)S(1)} fusion(bf16[64,64,128]{2,1,0:T(8,128)(2,1)S(1)} %get-tuple-element.159, f32[64,64]{1,0:T(8,128)S(1)} %broadcast_multiply_fusion.5), kind=kLoop, calls=%fused_computation.9.clone.1 | loop fusion | flops 2093056 | bytes 1081344 | tf_op jit(solution)/shard_map/while/body/eval_jaxpr/reduce_sum | solution.py:19
  96.9 3.4 %fusion.90 = bf16[2,64,64,128]{3,2,1,0:T(8,128)(2,1)} fusion(bf16[2,64,64,128]{3,2,1,0:T(8,128)(2,1)} %get-tuple-element.171, s32[]{:T(128)} %get-tuple-element.170, bf16[64,64,128]{2,1,0:T(8,128)(2,1)S(1)} %get-tuple-element.159, f32[64,64]{1,0:T(8,128)S(1)} %add_rsqrt_fusion.5, f32[64,64]{1,0:T(8,128)S(1)} %broadcast_multiply_fusion.5, ...), kind=kOutput, calls=%fused_computation.17.clone.1 | convolution fusion | flops 1081606144 | bytes 3473920 | tf_op jit(solution)/shard_map/while/body/eval_jaxpr/rck,kp->rcp/dot_general | solution.py:95
  (34 shorter events, 0.2 us)
Async XLA Ops:
  0.6 72.8 %copy-start = (bf16[1024,1024]{1,0:T(8,128)(2,1)S(1)}, bf16[1024,1024]{1,0:T(8,128)(2,1)}, u32[]{:S(2)}) copy-start(bf16[1024,1024]{1,0:T(8,128)(2,1)} %param.17) | copy-start | bytes 6291460
  0.6 2.9 %copy-start.1 = (bf16[128,64,128]{2,1,0:T(8,128)(2,1)S(1)}, bf16[128,64,128]{2,1,0:T(8,128)(2,1)}, u32[]{:S(2)}) copy-start(bf16[128,64,128]{2,1,0:T(8,128)(2,1)} %param.13) | copy-start | bytes 6291460
  6.4 3.4 %copy-start.7 = (bf16[128,32]{0,1:T(8,128)(2,1)S(1)}, bf16[128,32]{0,1:T(8,128)(2,1)}, u32[]{:S(2)}) copy-start(bf16[128,32]{0,1:T(8,128)(2,1)} %param.15) | copy-start | bytes 24580
  9.7 9.7 %copy-start.3 = (bf16[128,1024]{1,0:T(8,128)(2,1)S(1)}, bf16[128,1024]{1,0:T(8,128)(2,1)}, u32[]{:S(2)}) copy-start(bf16[128,1024]{1,0:T(8,128)(2,1)} %param.12) | copy-start | bytes 786436
  12.2 22.4 %all-to-all-start = ((bf16[32,128,64]{1,2,0:T(8,128)(2,1)}), bf16[32,128,64]{1,2,0:T(8,128)(2,1)}, u32[]{:S(2)}, u32[]{:S(2)}) async-start(bf16[32,128,64]{1,2,0:T(8,128)(2,1)} %copy.31), calls=%async_computation | async-start | bytes 1048576 | tf_op jit(solution)/shard_map/all_to_all | solution.py:42
  19.8 14.7 %copy-start.8 = (s32[512]{0:T(512)S(1)}, s32[512]{0:T(512)}, u32[]{:S(2)}) copy-start(s32[512]{0:T(512)} %param.14) | copy-start | bytes 6148
  21.9 0.7 copy-start.4
  41.0 33.3 %copy-start.9 = (bf16[1024,128]{1,0:T(8,128)(2,1)S(1)}, bf16[1024,128]{1,0:T(8,128)(2,1)}, u32[]{:S(2)}) copy-start(bf16[1024,128]{1,0:T(8,128)(2,1)} %param.18) | copy-start | bytes 786436
  41.9 43.3 %copy-start.6 = (bf16[128,128]{1,0:T(8,128)(2,1)S(1)}, bf16[128,128]{1,0:T(8,128)(2,1)}, u32[]{:S(2)}) copy-start(bf16[128,128]{1,0:T(8,128)(2,1)} %param.19) | copy-start | bytes 98308
  41.9 43.3 %copy-start.10 = (bf16[128,512]{1,0:T(8,128)(2,1)S(1)}, bf16[128,512]{1,0:T(8,128)(2,1)}, u32[]{:S(2)}) copy-start(bf16[128,512]{1,0:T(8,128)(2,1)} %param.20) | copy-start | bytes 393220
  41.9 43.3 %copy-start.11 = (bf16[512,128]{1,0:T(8,128)(2,1)S(1)}, bf16[512,128]{1,0:T(8,128)(2,1)}, u32[]{:S(2)}) copy-start(bf16[512,128]{1,0:T(8,128)(2,1)} %param.21) | copy-start | bytes 393220
  74.0 11.2 %copy-start.5 = (bf16[128,1024]{1,0:T(8,128)(2,1)}, bf16[128,1024]{1,0:T(8,128)(2,1)S(1)}, u32[]{:S(2)}) copy-start(bf16[128,1024]{1,0:T(8,128)(2,1)S(1)} %get-tuple-element.103) | copy-start | bytes 786436
  85.2 1.6 %copy-start.2 = (bf16[2,64,64,128]{3,2,1,0:T(8,128)(2,1)S(1)}, bf16[2,64,64,128]{3,2,1,0:T(8,128)(2,1)}, u32[]{:S(2)}) copy-start(bf16[2,64,64,128]{3,2,1,0:T(8,128)(2,1)} %get-tuple-element.181) | copy-start | bytes 6291460 | tf_op jit(solution)/shard_map/while
  92.8 1.6 %copy-start.2 = (bf16[2,64,64,128]{3,2,1,0:T(8,128)(2,1)S(1)}, bf16[2,64,64,128]{3,2,1,0:T(8,128)(2,1)}, u32[]{:S(2)}) copy-start(bf16[2,64,64,128]{3,2,1,0:T(8,128)(2,1)} %get-tuple-element.181) | copy-start | bytes 6291460 | tf_op jit(solution)/shard_map/while
where the time goes:
time: 101 us; the launch traced here: 100 us
  blocking collectives  53.1 us (53%)
  other arithmetic  15.9 us (16%)
  matrix products  15.5 us (15%)
  local copies, waits for them, and re-layouts  7.51 us (7%)
  starting transfers between devices  7.28 us (7%)
    all_gather x1, blocking collectives, per_device(): whole_heads = lax.all_gather(mixed, 'cols', axis=1, tiled=True)  31.5 us
    psum x1, blocking collectives, from_root(): return lax.psum(jnp.where(mine, value, jnp.zeros_like(value)), axis)  10.3 us
    all_to_all x1, starting transfers between devices, per_device(): lax.all_to_all(bias_local, 'cols', split_axis=0, concat_axis=2, tiled=True)  7.28 us
    dot_general x2, matrix products, update_block(): jnp.einsum('rck,kp->rcp', hidden, w_down, preferred_element_type=jnp.floa...  6.75 us
    all_gather x1, blocking collectives, per_device(): lax.all_gather(value_local, 'rows', axis=0, tiled=True)  5.88 us
    reduce_sum x5, other arithmetic, layer_norm(): jnp.mean(centred * centred, -1, keepdims=True) + epsilon  5.77 us
    all_gather x1, blocking collectives, per_device(): lax.all_gather(key_local, 'rows', axis=0, tiled=True)  5.43 us
    convert_element_type x1, other arithmetic, per_device(): normed_pair = layer_norm(pair).astype(jnp.bfloat16)  3.36 us
  transfers between devices with their start and end apart: 1, of which 0 were waited for; matrix products, arithmetic and copies ran while one was open for 3% of the time, Pallas kernels for 0%

commit v1 on v0

v1 whole, which is shorter than its diff:
```python
import functools
import math

import jax
import jax.numpy as jnp
from jax import lax
from jax.experimental import pallas as pl
from jax.experimental.pallas import tpu as pltpu
from jax.sharding import PartitionSpec as P

epsilon = 1e-05


def enter(axes):
    barrier = pltpu.get_barrier_semaphore()
    total = 0
    for axis, size in axes:
        me = lax.axis_index(axis)
        for step in range(1, size):
            pl.semaphore_signal(
                barrier,
                inc=1,
                device_id={axis: lax.rem(me + step, size)},
                device_id_type=pl.DeviceIdType.MESH,
            )
        total += size - 1
    pl.semaphore_wait(barrier, total)


def spread(axis, size, source, landing, send_sems, recv_sems):
    me = lax.axis_index(axis)
    copies = []
    for step in range(1, size):
        copy = pltpu.make_async_remote_copy(
            src_ref=source,
            dst_ref=landing.at[me],
            send_sem=send_sems.at[step - 1],
            recv_sem=recv_sems.at[step - 1],
            device_id={axis: lax.rem(me + step, size)},
            device_id_type=pl.DeviceIdType.MESH,
        )
        copy.start()
        copies.append(copy)
    return copies


def gather_kernel(axis, size, source, gathered, send_sems, recv_sems, own_sem):
    enter([(axis, size)])
    copies = spread(axis, size, source, gathered, send_sems, recv_sems)
    own = pltpu.make_async_copy(source, gathered.at[lax.axis_index(axis)], own_sem)
    own.start()
    own.wait()
    for copy in copies:
        copy.wait()


def gather(values, axis, size, collective_id):
    return pl.pallas_call(
        functools.partial(gather_kernel, axis, size),
        out_shape=jax.ShapeDtypeStruct((size, *values.shape), values.dtype),
        in_specs=[pl.BlockSpec(memory_space=pltpu.VMEM)],
        out_specs=pl.BlockSpec(memory_space=pltpu.VMEM),
        scratch_shapes=[
            pltpu.SemaphoreType.DMA((size - 1,)),
            pltpu.SemaphoreType.DMA((size - 1,)),
            pltpu.SemaphoreType.DMA,
        ],
        compiler_params=pltpu.CompilerParams(collective_id=collective_id, has_side_effects=True),
        name="gather_" + axis,
    )(values)


def single_kernel(
    row_size, col_size, tile_cols,
    mixed, single, w_out, w_factors, single_out, left_out, right_out,
    gathered, factor_right, send_sems, recv_sems, row_send, row_recv, own_sem,
):
    enter([("cols", col_size), ("rows", row_size)])
    tile_rows, width = mixed.shape
    me_col = lax.axis_index("cols")
    me_row = lax.axis_index("rows")
    copies = spread("cols", col_size, mixed, gathered, send_sems, recv_sems)
    own = pltpu.make_async_copy(mixed, gathered.at[me_col], own_sem)
    own.start()
    own.wait()
    for copy in copies:
        copy.wait()
    whole = jnp.concatenate([gathered[part] for part in range(col_size)], axis=1)
    total = jnp.dot(whole, w_out[...], preferred_element_type=jnp.float32)
    updated = (single[...].astype(jnp.float32) + total).astype(jnp.bfloat16)
    single_out[...] = updated
    normed = layer_norm(updated).astype(jnp.bfloat16)
    factors = jnp.dot(normed, w_factors[...], preferred_element_type=jnp.float32)
    factors = factors.astype(jnp.bfloat16).astype(jnp.float32)
    half = factors.shape[1] // 2
    swapped = jnp.concatenate([factors[:, half:], factors[:, :half]], axis=1)
    lower = lax.broadcasted_iota(jnp.int32, factors.shape, 1) < half
    left_out[...] = jnp.where(lower, factors, swapped)
    factor_right[...] = jnp.where(lower, swapped, factors).astype(jnp.bfloat16)
    first = me_col * tile_cols
    owner = first // tile_rows
    offset = pl.multiple_of(first - owner * tile_rows, tile_cols)
    piece = factor_right.at[pl.ds(offset, tile_cols)]

    @pl.when(me_row == owner)
    def _():
        local = pltpu.make_async_copy(piece, right_out, own_sem)
        local.start()
        sends = []
        for step in range(1, row_size):
            send = pltpu.make_async_remote_copy(
                src_ref=piece,
                dst_ref=right_out,
                send_sem=row_send.at[step - 1],
                recv_sem=row_recv,
                device_id={"rows": lax.rem(me_row + step, row_size)},
                device_id_type=pl.DeviceIdType.MESH,
            )
            send.start()
            sends.append(send)
        local.wait()
        for send in sends:
            send.wait_send()

    @pl.when(me_row != owner)
    def _():
        pltpu.make_async_remote_copy(
            src_ref=piece,
            dst_ref=right_out,
            send_sem=row_send.at[0],
            recv_sem=row_recv,
            device_id={"rows": lax.rem(me_row + 1, row_size)},
            device_id_type=pl.DeviceIdType.MESH,
        ).wait_recv()


def update_single(mixed, single, w_out, w_factors, row_size, col_size, tile_cols):
    tile_rows, width = single.shape
    wide = w_factors.shape[1]
    return pl.pallas_call(
        functools.partial(single_kernel, row_size, col_size, tile_cols),
        out_shape=(
            jax.ShapeDtypeStruct((tile_rows, width), jnp.bfloat16),
            jax.ShapeDtypeStruct((tile_rows, wide), jnp.float32),
            jax.ShapeDtypeStruct((tile_cols, wide), jnp.bfloat16),
        ),
        in_specs=[pl.BlockSpec(memory_space=pltpu.VMEM)] * 4,
        out_specs=[pl.BlockSpec(memory_space=pltpu.VMEM)] * 3,
        scratch_shapes=[
            pltpu.VMEM((col_size, *mixed.shape), jnp.bfloat16),
            pltpu.VMEM((tile_rows, wide), jnp.bfloat16),
            pltpu.SemaphoreType.DMA((col_size - 1,)),
            pltpu.SemaphoreType.DMA((col_size - 1,)),
            pltpu.SemaphoreType.DMA((row_size - 1,)),
            pltpu.SemaphoreType.DMA,
            pltpu.SemaphoreType.DMA,
        ],
        compiler_params=pltpu.CompilerParams(collective_id=2, has_side_effects=True),
        name="update_single",
    )(mixed, single, w_out, w_factors)


def norm_kernel(values, normed):
    normed[...] = layer_norm(values[...]).astype(jnp.bfloat16)


def norm_rows(values, block):
    spec = pl.BlockSpec((block, values.shape[1]), lambda step: (step, 0))
    return pl.pallas_call(
        norm_kernel,
        out_shape=jax.ShapeDtypeStruct(values.shape, jnp.bfloat16),
        grid=(values.shape[0] // block,),
        in_specs=[spec],
        out_specs=spec,
        name="norm_pair",
    )(values)


def pair_kernel(pair, left, right, w_pairout, w_up, w_down, updated):
    block_rows, tile_cols, wide = pair.shape
    left_wide = left[...][:, None, :]
    right_wide = right[...].astype(jnp.float32)[None, :, :]
    lower = lax.broadcasted_iota(jnp.int32, pair.shape, 2) < wide // 2
    paired = jnp.where(lower, left_wide * right_wide, left_wide - right_wide)
    paired = paired.astype(jnp.bfloat16).reshape(block_rows * tile_cols, wide)
    flat = pair[...].reshape(block_rows * tile_cols, wide).astype(jnp.float32)
    mid = flat + jnp.dot(paired, w_pairout[...], preferred_element_type=jnp.float32)
    mid = mid.astype(jnp.bfloat16)
    normed = layer_norm(mid).astype(jnp.bfloat16)
    hidden = jnp.dot(normed, w_up[...], preferred_element_type=jnp.float32)
    hidden = jnp.maximum(hidden, 0.0).astype(jnp.bfloat16)
    out = mid.astype(jnp.float32) + jnp.dot(
        hidden, w_down[...], preferred_element_type=jnp.float32
    )
    updated[...] = out.astype(jnp.bfloat16).reshape(pair.shape)


def update_pair(pair, left, right, w_pairout, w_up, w_down):
    tile_rows, tile_cols, wide = pair.shape
    block = math.gcd(tile_rows, max(8, 1024 // tile_cols))
    tile = pl.BlockSpec((block, tile_cols, wide), lambda step: (step, 0, 0))

    def whole(array):
        return pl.BlockSpec(array.shape, lambda step: (0, 0))

    return pl.pallas_call(
        pair_kernel,
        out_shape=jax.ShapeDtypeStruct(pair.shape, jnp.bfloat16),
        grid=(tile_rows // block,),
        in_specs=[
            tile,
            pl.BlockSpec((block, wide), lambda step: (step, 0)),
            whole(right),
            whole(w_pairout),
            whole(w_up),
            whole(w_down),
        ],
        out_specs=tile,
        name="update_pair",
    )(pair, left, right, w_pairout, w_up, w_down)


def layer_norm(values):
    values = values.astype(jnp.float32)
    centred = values - jnp.mean(values, -1, keepdims=True)
    return centred * lax.rsqrt(jnp.mean(centred * centred, -1, keepdims=True) + epsilon)


def per_device(
    row_size, col_size,
    single, pair, residue_mask, w_bias, w_project, w_out, w_factors, w_pairout, w_up, w_down
):
    tile_rows = pair.shape[0]
    tile_cols = pair.shape[1]
    normed_pair = norm_rows(
        pair.reshape(tile_rows * tile_cols, pair.shape[2]), math.gcd(tile_rows * tile_cols, 1024)
    ).reshape(pair.shape)
    bias_local = jnp.einsum(
        "rcp,ph->hrc", normed_pair, w_bias, preferred_element_type=jnp.float32
    ).astype(jnp.bfloat16)
    normed_single = layer_norm(single).astype(jnp.bfloat16)
    projected = jnp.einsum(
        "rs,fsc->frc", normed_single, w_project, preferred_element_type=jnp.float32
    )
    query_rows = projected[0].astype(jnp.bfloat16)
    key_local = projected[1].astype(jnp.bfloat16)
    value_local = projected[2].astype(jnp.bfloat16)
    gate_values = jax.nn.sigmoid(projected[3])
    bias_heads = lax.all_to_all(bias_local, "cols", split_axis=0, concat_axis=2, tiled=True)
    both = gather(jnp.concatenate([key_local, value_local], 1), "rows", row_size, 1)
    both = both.reshape(row_size * tile_rows, both.shape[2])
    key_rows, value_rows = both[:, : key_local.shape[1]], both[:, key_local.shape[1] :]
    heads_here = bias_heads.shape[0]
    head_width = query_rows.shape[1] // heads_here
    residues = key_rows.shape[0]
    query_split = query_rows.reshape(tile_rows, heads_here, head_width)
    key_split = key_rows.reshape(residues, heads_here, head_width)
    value_split = value_rows.reshape(residues, heads_here, head_width)
    score_scale = 1.0 / math.sqrt(head_width)
    scores = jnp.einsum(
        "rhd,lhd->hrl", query_split, key_split, preferred_element_type=jnp.float32
    ) * score_scale + bias_heads.astype(jnp.float32)
    key_valid = (residue_mask > 0)[None, None, :]
    scores = jnp.where(key_valid, scores, -jnp.inf)
    weights = jax.nn.softmax(scores, axis=-1).astype(jnp.bfloat16)
    attended = jnp.einsum("hrl,lhd->rhd", weights, value_split, preferred_element_type=jnp.float32)
    attended = attended.reshape(tile_rows, heads_here * head_width)
    mixed = (attended * gate_values).astype(jnp.bfloat16)
    single_out, left, right = update_single(
        mixed, single, w_out, w_factors, row_size, col_size, tile_cols
    )
    return (single_out, update_pair(pair, left, right, w_pairout, w_up, w_down))


def solution(mesh):
    return jax.shard_map(
        functools.partial(per_device, mesh.shape["rows"], mesh.shape["cols"]),
        mesh=mesh,
        in_specs=(
            P("rows", None),
            P("rows", "cols", None),
            P(),
            P(),
            P(None, None, "cols"),
            P(),
            P(),
            P(),
            P(),
            P(),
        ),
        out_specs=(P("rows", None), P("rows", "cols", None)),
        check_vma=False,
    )
```

time: 101 us -> 63.5 us (0.63)
  blocking collectives: 53.1 us -> 0 us
  Pallas kernels: 0 us -> 39.4 us
  other arithmetic: 15.9 us -> 2.08 us
  matrix products: 15.5 us -> 5 us
  waiting for transfers between devices: 0.01 us -> 4.26 us
  local copies, waits for them, and re-layouts: 7.51 us -> 4.25 us
    all_gather x3 -> x0, blocking collectives: 42.8 us -> none  [the longest x1 31.5 us: per_device(): whole_heads = lax.all_gather(mixed, 'cols', axis=1, tiled=True)]
    pallas_call x0 -> x4, Pallas kernels: none -> 39.4 us  [the longest x1 13.1 us: update_single(): pl.pallas_call(functools.partial(single_kernel, row_size, col_size, tile_...]
    psum x1 -> x0, blocking collectives: 10.3 us -> none  [from_root(): return lax.psum(jnp.where(mine, value, jnp.zeros_like(value)), axis)]
    dot_general x6 -> x0, matrix products: 10 us -> none  [the longest x2 6.75 us: update_block(): jnp.einsum('rck,kp->rcp', hidden, w_down, preferred_element_type=jnp.floa...]
    reduce_sum x5 -> x1, other arithmetic: 5.77 us -> 0.22 us  [layer_norm(): jnp.mean(centred * centred, -1, keepdims=True) + epsilon]
    all_to_all x1, waiting for transfers between devices: 0.01 us -> 4.26 us  [per_device(): lax.all_to_all(bias_local, 'cols', split_axis=0, concat_axis=2, tiled=True)]
    convert_element_type x5 -> x0, other arithmetic: 3.38 us -> none  [the longest x1 3.36 us: per_device(): normed_pair = layer_norm(pair).astype(jnp.bfloat16)]
    reduce_sum x2 -> x1, other arithmetic: 3.02 us -> 0.12 us  [layer_norm(): centred = values - jnp.mean(values, -1, keepdims=True)]
  transfers between devices with their start and end apart: 1 -> 1, of which waited for: 0 -> 1; matrix products, arithmetic and copies ran while one was open for 3% -> 6% of each run, Pallas kernels for 0% -> 10%
where the time goes in v1:
time: 63.5 us; the launch traced here: 63 us
  Pallas kernels  39.4 us (62%)
  starting transfers between devices  7.28 us (11%)
  matrix products  5 us (8%)
  waiting for transfers between devices  4.26 us (7%)
  local copies, waits for them, and re-layouts  4.25 us (7%)
  other arithmetic  2.08 us (3%)
  between operations  0.81 us (1%)
    pallas_call x1, Pallas kernels, update_single(): pl.pallas_call(functools.partial(single_kernel, row_size, col_size, tile_...  13.1 us
    pallas_call x1, Pallas kernels, update_pair(): pl.pallas_call(pair_kernel, out_shape=jax.ShapeDtypeStruct(pair.shape, jn...  12.7 us
    all_to_all x1, starting transfers between devices, per_device(): lax.all_to_all(bias_local, 'cols', split_axis=0, concat_axis=2, tiled=True)  7.28 us
    pallas_call x1, Pallas kernels, norm_rows(): pl.pallas_call(norm_kernel, out_shape=jax.ShapeDtypeStruct(values.shape,...  6.91 us
    pallas_call x1, Pallas kernels, gather(): pl.pallas_call(functools.partial(gather_kernel, axis, size), out_shape=ja...  6.56 us
    all_to_all x1, waiting for transfers between devices, per_device(): lax.all_to_all(bias_local, 'cols', split_axis=0, concat_axis=2, tiled=True)  4.26 us
    dot_general x1, matrix products, per_device(): jnp.einsum('rcp,ph->hrc', normed_pair, w_bias, preferred_element_type=jnp...  3.08 us
  transfers between devices with their start and end apart: 1, of which 1 were waited for; matrix products, arithmetic and copies ran while one was open for 6% of the time, Pallas kernels for 10%

profile of v1, /device:TPU:0, one launch (start us, length us, event | category | flops | bytes accessed | tf_op | source)
XLA Modules:
  0.0 63.0 jit_solution(4962976992004762761)
XLA Ops:
  0.6 0.0 copy-start
  0.6 6.9 %norm_pair.1 = bf16[8192,128]{1,0:T(8,128)(2,1)} custom-call(bf16[8192,128]{1,0:T(8,128)(2,1)} %bitcast.40), custom_call_target="tpu_custom_call" | custom-call | tf_op jit(solution)/shard_map/norm_pair/pallas_call | solution.py:169
  7.6 0.0 copy-done
  7.6 0.0 copy-start.1
  7.6 0.0 copy-start.2
  7.6 3.1 %fusion.7 = bf16[32,128,64]{1,0,2:T(8,128)(2,1)S(1)} fusion(bf16[128,64,128]{2,1,0:T(8,128)(2,1)} %bitcast.39, bf16[128,32]{0,1:T(8,128)(2,1)S(1)} %copy-done), kind=kOutput, calls=%fused_computation.8 | convolution fusion | flops 67371008 | bytes 2629632 | tf_op jit(solution)/shard_map/rcp,ph->hrc/dot_general | solution.py:238
  10.7 1.0 %copy.44 = bf16[32,128,64]{1,2,0:T(8,128)(2,1)} copy(bf16[32,128,64]{1,0,2:T(8,128)(2,1)S(1)} %fusion.7) | data formatting | bytes 1048576 | tf_op jit(solution)/shard_map/convert_element_type | solution.py:240
  11.7 7.3 %all-to-all-start = ((bf16[32,128,64]{1,2,0:T(8,128)(2,1)}), bf16[32,128,64]{1,2,0:T(8,128)(2,1)S(1)}, u32[]{:S(2)}, u32[]{:S(2)}) async-start(bf16[32,128,64]{1,2,0:T(8,128)(2,1)} %copy.44), calls=%async_computation | async-start | bytes 1048576 | tf_op jit(solution)/shard_map/all_to_all | solution.py:249
  18.9 0.0 copy-done.1
  18.9 0.1 convert_reduce_fusion
  19.1 0.2 fusion.12
  19.3 0.0 copy-done.2
  19.3 0.5 copy.38
  19.9 0.0 copy-start.4
  19.9 0.5 fusion.15
  20.4 0.1 copy.39
  20.6 0.6 %pad_maximum_fusion.source = bf16[128,256]{1,0:T(8,128)(2,1)} fusion(bf16[128,128]{1,0:T(8,128)(2,1)S(1)} %get-tuple-element.11, bf16[128,128]{1,0:T(8,128)(2,1)S(1)} %get-tuple-element.12), kind=kLoop, calls=%fused_computation.27 | loop fusion | flops 131072 | bytes 131072 | tf_op jit(solution)/shard_map/concatenate | solution.py:250
  21.2 6.6 %gather_rows.1 = bf16[4,128,256]{2,1,0:T(8,128)(2,1)} custom-call(bf16[128,256]{1,0:T(8,128)(2,1)} %pad_maximum_fusion.source), custom_call_target="tpu_custom_call" | custom-call | tf_op jit(solution)/shard_map/gather_rows/pallas_call | solution.py:58
  27.8 1.0 %fusion.27 = (bf16[512,128]{1,0:T(8,128)(2,1)S(1)}, bf16[512,128]{1,0:T(8,128)(2,1)S(1)}) fusion(bf16[512,256]{1,0:T(8,128)(2,1)} %bitcast.45), kind=kLoop, calls=%fused_computation.37 | loop fusion | bytes 524288 | tf_op jit(solution)/shard_map/slice | solution.py:252
  28.8 0.1 copy.42
  28.9 0.1 copy.41
  29.0 0.1 copy.40
  29.1 0.0 copy-done.4
  29.2 4.3 %all-to-all-done = bf16[32,128,64]{1,2,0:T(8,128)(2,1)S(1)} async-done(((bf16[32,128,64]{1,2,0:T(8,128)(2,1)}), bf16[32,128,64]{1,2,0:T(8,128)(2,1)S(1)}, u32[]{:S(2)}, u32[]{:S(2)}) %all-to-all-start) | async-done | bytes 524320 | tf_op jit(solution)/shard_map/all_to_all | solution.py:249
  33.4 0.1 convert_bitcast_fusion
  33.5 0.1 copy.45
  33.6 0.3 copy.46
  34.0 0.3 fusion.6
  34.3 0.3 fusion.29
  34.6 1.0 %fusion.14 = f32[4,32,128]{2,1,0:T(8,128)S(1)} fusion(bf16[512,4,32]{0,2,1:T(8,128)(2,1)S(1)} %bitcast.49, f32[4,128]{1,0:T(4,128)S(1)} %fusion.29, f32[4,128,512]{2,1,0:T(8,128)S(1)} %fusion.6), kind=kOutput, calls=%fused_computation.17 | convolution fusion | flops 17564672 | bytes 1247232 | tf_op jit(solution)/shard_map/hrl,lhd->rhd/dot_general | solution.py:266
  35.7 0.1 copy.47
  35.8 0.7 %fusion.24.mixed = bf16[128,128]{1,0:T(8,128)(2,1)} fusion(f32[128,128]{1,0:T(8,128)S(1)} %copy.47, f32[4,128,128]{2,1,0:T(8,128)S(1)} %bitcast.44), kind=kLoop, calls=%fused_computation.28 | loop fusion | flops 81920 | bytes 163840 | tf_op jit(solution)/shard_map/convert_element_type | solution.py:268
  36.4 13.1 %update_single.1 = (bf16[128,1024]{1,0:T(8,128)(2,1)}, f32[128,128]{1,0:T(8,128)}, bf16[64,128]{1,0:T(8,128)(2,1)}) custom-call(bf16[128,128]{1,0:T(8,128)(2,1)} %fusion.24.mixed, bf16[128,1024]{1,0:T(8,128)(2,1)} %single.1, bf16[1024,1024]{1,0:T(8,128)(2,1)} %w_out.1, bf16[1024,128]{1,0:T(8,128)(2,1)} %w_factors.1), custom_call_target="tpu_custom_call" | custom-call | tf_op jit(solution)/shard_map/update_single/pallas_call | solution.py:140
  49.6 0.0 copy-start.3
  49.6 12.7 %update_pair.1 = bf16[128,64,128]{2,1,0:T(8,128)(2,1)} custom-call(bf16[128,64,128]{2,1,0:T(8,128)(2,1)} %pair.1, f32[128,128]{1,0:T(8,128)} %get-tuple-element.6.left, bf16[64,128]{1,0:T(8,128)(2,1)} %get-tuple-element.7.right, bf16[128,128]{1,0:T(8,128)(2,1)} %w_pairout.1, bf16[128,512]{1,0:T(8,128)(2,1)} %w_up.1, bf16[512,128]{1,0:T(8,128)(2,1)} %w_down.1), custom_call_target="tpu_custom_call" | custom-call | tf_op jit(solution)/shard_map/update_pair/pallas_call | solution.py:206
  62.3 0.0 copy-done.3
  62.3 0.7 %copy.53 = bf16[128,1024]{1,0:T(8,128)(2,1)} copy(bf16[128,1024]{1,0:T(8,128)(2,1)S(1)} %copy-done.3) | data formatting | bytes 524288
  (5 shorter events, 0.1 us)
Async XLA Ops:
  0.6 6.9 %copy-start = (bf16[128,32]{0,1:T(8,128)(2,1)S(1)}, bf16[128,32]{0,1:T(8,128)(2,1)}, u32[]{:S(2)}) copy-start(bf16[128,32]{0,1:T(8,128)(2,1)} %param.13) | copy-start | bytes 24580
  7.6 11.4 %copy-start.1 = (bf16[128,1024]{1,0:T(8,128)(2,1)S(1)}, bf16[128,1024]{1,0:T(8,128)(2,1)}, u32[]{:S(2)}) copy-start(bf16[128,1024]{1,0:T(8,128)(2,1)} %single.1) | copy-start | bytes 786436
  7.6 11.7 %copy-start.2 = (bf16[4,1024,128]{2,1,0:T(8,128)(2,1)S(1)}, bf16[4,1024,128]{2,1,0:T(8,128)(2,1)}, u32[]{:S(2)}) copy-start(bf16[4,1024,128]{2,1,0:T(8,128)(2,1)} %param.14) | copy-start | bytes 3145732
  11.7 21.8 %all-to-all-start = ((bf16[32,128,64]{1,2,0:T(8,128)(2,1)}), bf16[32,128,64]{1,2,0:T(8,128)(2,1)S(1)}, u32[]{:S(2)}, u32[]{:S(2)}) async-start(bf16[32,128,64]{1,2,0:T(8,128)(2,1)} %copy.44), calls=%async_computation | async-start | bytes 1048576 | tf_op jit(solution)/shard_map/all_to_all | solution.py:249
  19.9 9.3 %copy-start.4 = (s32[512]{0:T(512)S(1)}, s32[512]{0:T(512)}, u32[]{:S(2)}) copy-start(s32[512]{0:T(512)} %param.12) | copy-start | bytes 6148
  49.6 12.8 %copy-start.3 = (bf16[128,1024]{1,0:T(8,128)(2,1)S(1)}, bf16[128,1024]{1,0:T(8,128)(2,1)}, u32[]{:S(2)}) copy-start(bf16[128,1024]{1,0:T(8,128)(2,1)} %get-tuple-element.15) | copy-start | bytes 786436

commit v2 on v1

--- a/solution.py
+++ b/solution.py
@@ -160,8 +160,22 @@
     )(mixed, single, w_out, w_factors)
 
 
+def matmul_norm(values):
+    wide = values.shape[1]
+    share = jnp.full((2 * wide, wide), 1.0 / wide, jnp.bfloat16)
+    mean = jnp.dot(values, share[:wide], preferred_element_type=jnp.float32)
+    centred = values.astype(jnp.float32) - mean
+    square = centred * centred
+    high = square.astype(jnp.bfloat16)
+    low = (square - high.astype(jnp.float32)).astype(jnp.bfloat16)
+    spread_out = jnp.dot(
+        jnp.concatenate([high, low], 1), share, preferred_element_type=jnp.float32
+    )
+    return (centred * lax.rsqrt(spread_out + epsilon)).astype(jnp.bfloat16)
+
+
 def norm_kernel(values, normed):
-    normed[...] = layer_norm(values[...]).astype(jnp.bfloat16)
+    normed[...] = matmul_norm(values[...])
 
 
 def norm_rows(values, block):
@@ -186,7 +200,7 @@
     flat = pair[...].reshape(block_rows * tile_cols, wide).astype(jnp.float32)
     mid = flat + jnp.dot(paired, w_pairout[...], preferred_element_type=jnp.float32)
     mid = mid.astype(jnp.bfloat16)
-    normed = layer_norm(mid).astype(jnp.bfloat16)
+    normed = matmul_norm(mid)
     hidden = jnp.dot(normed, w_up[...], preferred_element_type=jnp.float32)
     hidden = jnp.maximum(hidden, 0.0).astype(jnp.bfloat16)
     out = mid.astype(jnp.float32) + jnp.dot(

time: 63.5 us -> 62.5 us (0.984)
  Pallas kernels: 39.4 us -> 38.3 us
    pallas_call x1, Pallas kernels: 12.7 us -> 11.2 us  [update_pair(): pl.pallas_call(pair_kernel, out_shape=jax.ShapeDtypeStruct(pair.shape, jn...]
  transfers between devices with their start and end apart: 1 -> 1, of which waited for: 1 -> 1; matrix products, arithmetic and copies ran while one was open for 6% -> 6% of each run, Pallas kernels for 10% -> 11%
where the time goes in v2:
time: 62.5 us; the launch traced here: 62 us
  Pallas kernels  38.3 us (61%)
  starting transfers between devices  7.28 us (12%)
  matrix products  4.99 us (8%)
  waiting for transfers between devices  4.27 us (7%)
  local copies, waits for them, and re-layouts  4.25 us (7%)
  other arithmetic  2.08 us (3%)
  between operations  0.81 us (1%)
    pallas_call x1, Pallas kernels, update_single(): pl.pallas_call(functools.partial(single_kernel, row_size, col_size, tile_...  13.1 us
    pallas_call x1, Pallas kernels, update_pair(): pl.pallas_call(pair_kernel, out_shape=jax.ShapeDtypeStruct(pair.shape, jn...  11.2 us
    pallas_call x1, Pallas kernels, norm_rows(): pl.pallas_call(norm_kernel, out_shape=jax.ShapeDtypeStruct(values.shape,...  7.48 us
    all_to_all x1, starting transfers between devices, per_device(): lax.all_to_all(bias_local, 'cols', split_axis=0, concat_axis=2, tiled=True)  7.28 us
    pallas_call x1, Pallas kernels, gather(): pl.pallas_call(functools.partial(gather_kernel, axis, size), out_shape=ja...  6.56 us
    all_to_all x1, waiting for transfers between devices, per_device(): lax.all_to_all(bias_local, 'cols', split_axis=0, concat_axis=2, tiled=True)  4.27 us
    dot_general x1, matrix products, per_device(): jnp.einsum('rcp,ph->hrc', normed_pair, w_bias, preferred_element_type=jnp...  3.08 us
    unnamed x12, local copies, waits for them, and re-layouts  1.26 us
  transfers between devices with their start and end apart: 1, of which 1 were waited for; matrix products, arithmetic and copies ran while one was open for 6% of the time, Pallas kernels for 11%

profile of v2, /device:TPU:0, one launch (start us, length us, event | category | flops | bytes accessed | tf_op | source)
XLA Modules:
  0.0 62.0 jit_solution(652438604577849002)
XLA Ops:
  0.6 0.0 copy-start
  0.6 7.5 %norm_pair.1 = bf16[8192,128]{1,0:T(8,128)(2,1)} custom-call(bf16[8192,128]{1,0:T(8,128)(2,1)} %bitcast.40), custom_call_target="tpu_custom_call" | custom-call | tf_op jit(solution)/shard_map/norm_pair/pallas_call | solution.py:183
  8.1 0.0 copy-done
  8.1 0.0 copy-start.1
  8.1 0.0 copy-start.2
  8.1 3.1 %fusion.7 = bf16[32,128,64]{1,0,2:T(8,128)(2,1)S(1)} fusion(bf16[128,64,128]{2,1,0:T(8,128)(2,1)} %bitcast.39, bf16[128,32]{0,1:T(8,128)(2,1)S(1)} %copy-done), kind=kOutput, calls=%fused_computation.8 | convolution fusion | flops 67371008 | bytes 2629632 | tf_op jit(solution)/shard_map/rcp,ph->hrc/dot_general | solution.py:252
  11.2 1.0 %copy.44 = bf16[32,128,64]{1,2,0:T(8,128)(2,1)} copy(bf16[32,128,64]{1,0,2:T(8,128)(2,1)S(1)} %fusion.7) | data formatting | bytes 1048576 | tf_op jit(solution)/shard_map/convert_element_type | solution.py:254
  12.2 7.3 %all-to-all-start = ((bf16[32,128,64]{1,2,0:T(8,128)(2,1)}), bf16[32,128,64]{1,2,0:T(8,128)(2,1)S(1)}, u32[]{:S(2)}, u32[]{:S(2)}) async-start(bf16[32,128,64]{1,2,0:T(8,128)(2,1)} %copy.44), calls=%async_computation | async-start | bytes 1048576 | tf_op jit(solution)/shard_map/all_to_all | solution.py:263
  19.5 0.0 copy-done.1
  19.5 0.1 convert_reduce_fusion
  19.6 0.2 fusion.12
  19.9 0.0 copy-done.2
  19.9 0.5 copy.38
  20.4 0.0 copy-start.4
  20.4 0.5 fusion.15
  21.0 0.1 copy.39
  21.1 0.6 %pad_maximum_fusion.source = bf16[128,256]{1,0:T(8,128)(2,1)} fusion(bf16[128,128]{1,0:T(8,128)(2,1)S(1)} %get-tuple-element.11, bf16[128,128]{1,0:T(8,128)(2,1)S(1)} %get-tuple-element.12), kind=kLoop, calls=%fused_computation.27 | loop fusion | flops 131072 | bytes 131072 | tf_op jit(solution)/shard_map/concatenate | solution.py:264
  21.8 6.6 %gather_rows.1 = bf16[4,128,256]{2,1,0:T(8,128)(2,1)} custom-call(bf16[128,256]{1,0:T(8,128)(2,1)} %pad_maximum_fusion.source), custom_call_target="tpu_custom_call" | custom-call | tf_op jit(solution)/shard_map/gather_rows/pallas_call | solution.py:58
  28.3 1.0 %fusion.27 = (bf16[512,128]{1,0:T(8,128)(2,1)S(1)}, bf16[512,128]{1,0:T(8,128)(2,1)S(1)}) fusion(bf16[512,256]{1,0:T(8,128)(2,1)} %bitcast.45), kind=kLoop, calls=%fused_computation.37 | loop fusion | bytes 524288 | tf_op jit(solution)/shard_map/slice | solution.py:266
  29.3 0.1 copy.42
  29.5 0.1 copy.41
  29.6 0.1 copy.40
  29.7 0.0 copy-done.4
  29.7 4.3 %all-to-all-done = bf16[32,128,64]{1,2,0:T(8,128)(2,1)S(1)} async-done(((bf16[32,128,64]{1,2,0:T(8,128)(2,1)}), bf16[32,128,64]{1,2,0:T(8,128)(2,1)S(1)}, u32[]{:S(2)}, u32[]{:S(2)}) %all-to-all-start) | async-done | bytes 524320 | tf_op jit(solution)/shard_map/all_to_all | solution.py:263
  34.0 0.1 convert_bitcast_fusion
  34.1 0.1 copy.45
  34.2 0.3 copy.46
  34.5 0.3 fusion.6
  34.9 0.3 fusion.29
  35.2 1.0 %fusion.14 = f32[4,32,128]{2,1,0:T(8,128)S(1)} fusion(bf16[512,4,32]{0,2,1:T(8,128)(2,1)S(1)} %bitcast.49, f32[4,128]{1,0:T(4,128)S(1)} %fusion.29, f32[4,128,512]{2,1,0:T(8,128)S(1)} %fusion.6), kind=kOutput, calls=%fused_computation.17 | convolution fusion | flops 17564672 | bytes 1247232 | tf_op jit(solution)/shard_map/hrl,lhd->rhd/dot_general | solution.py:280
  36.2 0.1 copy.47
  36.4 0.7 %fusion.24.mixed = bf16[128,128]{1,0:T(8,128)(2,1)} fusion(f32[128,128]{1,0:T(8,128)S(1)} %copy.47, f32[4,128,128]{2,1,0:T(8,128)S(1)} %bitcast.44), kind=kLoop, calls=%fused_computation.28 | loop fusion | flops 81920 | bytes 163840 | tf_op jit(solution)/shard_map/convert_element_type | solution.py:282
  37.0 13.1 %update_single.1 = (bf16[128,1024]{1,0:T(8,128)(2,1)}, f32[128,128]{1,0:T(8,128)}, bf16[64,128]{1,0:T(8,128)(2,1)}) custom-call(bf16[128,128]{1,0:T(8,128)(2,1)} %fusion.24.mixed, bf16[128,1024]{1,0:T(8,128)(2,1)} %single.1, bf16[1024,1024]{1,0:T(8,128)(2,1)} %w_out.1, bf16[1024,128]{1,0:T(8,128)(2,1)} %w_factors.1), custom_call_target="tpu_custom_call" | custom-call | tf_op jit(solution)/shard_map/update_single/pallas_call | solution.py:140
  50.2 0.0 copy-start.3
  50.2 11.2 %update_pair.1 = bf16[128,64,128]{2,1,0:T(8,128)(2,1)} custom-call(bf16[128,64,128]{2,1,0:T(8,128)(2,1)} %pair.1, f32[128,128]{1,0:T(8,128)} %get-tuple-element.6.left, bf16[64,128]{1,0:T(8,128)(2,1)} %get-tuple-element.7.right, bf16[128,128]{1,0:T(8,128)(2,1)} %w_pairout.1, bf16[128,512]{1,0:T(8,128)(2,1)} %w_up.1, bf16[512,128]{1,0:T(8,128)(2,1)} %w_down.1), custom_call_target="tpu_custom_call" | custom-call | tf_op jit(solution)/shard_map/update_pair/pallas_call | solution.py:220
  61.3 0.0 copy-done.3
  61.3 0.7 %copy.53 = bf16[128,1024]{1,0:T(8,128)(2,1)} copy(bf16[128,1024]{1,0:T(8,128)(2,1)S(1)} %copy-done.3) | data formatting | bytes 524288
  (5 shorter events, 0.0 us)
Async XLA Ops:
  0.6 7.5 %copy-start = (bf16[128,32]{0,1:T(8,128)(2,1)S(1)}, bf16[128,32]{0,1:T(8,128)(2,1)}, u32[]{:S(2)}) copy-start(bf16[128,32]{0,1:T(8,128)(2,1)} %param.13) | copy-start | bytes 24580
  8.1 11.4 %copy-start.1 = (bf16[128,1024]{1,0:T(8,128)(2,1)S(1)}, bf16[128,1024]{1,0:T(8,128)(2,1)}, u32[]{:S(2)}) copy-start(bf16[128,1024]{1,0:T(8,128)(2,1)} %single.1) | copy-start | bytes 786436
  8.1 11.7 %copy-start.2 = (bf16[4,1024,128]{2,1,0:T(8,128)(2,1)S(1)}, bf16[4,1024,128]{2,1,0:T(8,128)(2,1)}, u32[]{:S(2)}) copy-start(bf16[4,1024,128]{2,1,0:T(8,128)(2,1)} %param.14) | copy-start | bytes 3145732
  12.2 21.8 %all-to-all-start = ((bf16[32,128,64]{1,2,0:T(8,128)(2,1)}), bf16[32,128,64]{1,2,0:T(8,128)(2,1)S(1)}, u32[]{:S(2)}, u32[]{:S(2)}) async-start(bf16[32,128,64]{1,2,0:T(8,128)(2,1)} %copy.44), calls=%async_computation | async-start | bytes 1048576 | tf_op jit(solution)/shard_map/all_to_all | solution.py:263
  20.4 9.3 %copy-start.4 = (s32[512]{0:T(512)S(1)}, s32[512]{0:T(512)}, u32[]{:S(2)}) copy-start(s32[512]{0:T(512)} %param.12) | copy-start | bytes 6148
  50.2 11.2 %copy-start.3 = (bf16[128,1024]{1,0:T(8,128)(2,1)S(1)}, bf16[128,1024]{1,0:T(8,128)(2,1)}, u32[]{:S(2)}) copy-start(bf16[128,1024]{1,0:T(8,128)(2,1)} %get-tuple-element.15) | copy-start | bytes 786436
